TPU v7x, 128 devices: a whole 4x4x4 slice. The times are simulated.
128 devices in a mesh: member: 1, lon: 16 (over z, y), lat: 8 (over x, core).
Axes of the slice: x: 4, y: 4, z: 4, core: 2. Of those that a mesh axis runs over, the one named last changes fastest.
Arguments:
- field_in: float32 [8, 256, 192, 384], P('member', None, 'lat', 'lon')
- fwd_table: float32 [128, 128, 192], replicated
- inv_table: float32 [128, 128, 192], replicated
- mix_weights: float32 [128, 256, 256, 2], replicated
Outputs:
- output: float32 [8, 256, 192, 384], P('member', None, 'lat', 'lon')
All inputs are finite; a program needn't handle non-finite values.
Results may differ from a plain program's by a relative error of at most 0.00401796.
Values are sent between devices in bfloat16 or wider.
A program may use at most 1 GiB of HBM per device.

v0:
```python
import math
import jax
import jax.numpy as jnp
from jax import lax
from jax.sharding import PartitionSpec as P


def dft_tables(lon_points, wave_ids):
    lon_ids = jnp.arange(lon_points)
    phase_arg = (2.0 * math.pi / lon_points) * ((lon_ids[:, None] * wave_ids[None, :]) % lon_points).astype(jnp.float32)
    cos_val = jnp.cos(phase_arg)
    sin_val = jnp.sin(phase_arg)
    weight_m = jnp.where(wave_ids == 0, 1.0, 2.0).astype(jnp.float32)
    fwd_dft = jnp.stack([cos_val, -sin_val], axis=1).astype(jnp.bfloat16)
    inv_dft = jnp.stack([(weight_m * cos_val).T, (-weight_m * sin_val).T], axis=0).astype(jnp.bfloat16)
    return fwd_dft, inv_dft


def solution(mesh):
    lon_count = mesh.shape['lon']
    grid_spec = P('member', None, 'lat', 'lon')

    def local_layer(field_in, fwd_table, inv_table, mix_weights):
        lon_points = field_in.shape[3] * lon_count
        degrees = fwd_table.shape[1]
        fwd_dft, inv_dft = dft_tables(lon_points, jnp.arange(degrees))
        grid_bf = field_in.astype(jnp.bfloat16)
        lon_full = lax.all_to_all(grid_bf, 'lon', 1, 3, tiled=True)
        spec_all = jnp.einsum('sctj,jrm->sctrm', lon_full, fwd_dft, preferred_element_type=jnp.float32).astype(jnp.bfloat16)
        spec_loc = lax.all_to_all(spec_all, 'lat', 4, 2, tiled=True)
        coef_loc = jnp.einsum('mlt,sctrm->sclrm', fwd_table.astype(jnp.bfloat16), spec_loc, preferred_element_type=jnp.float32).astype(jnp.bfloat16)
        coef_chan = lax.all_to_all(coef_loc, 'lon', 2, 1, tiled=True)
        w_bf = mix_weights.astype(jnp.bfloat16)
        w_re = w_bf[..., 0]
        w_im = w_bf[..., 1]
        w_block = jnp.stack([jnp.stack([w_re, -w_im], axis=-1), jnp.stack([w_im, w_re], axis=-1)], axis=2)
        mixed_chan = jnp.einsum('loqir,silrm->solqm', w_block, coef_chan, preferred_element_type=jnp.float32).astype(jnp.bfloat16)
        mixed_loc = lax.all_to_all(mixed_chan, 'lon', 1, 2, tiled=True)
        back_loc = jnp.einsum('mlt,sclrm->sctrm', inv_table.astype(jnp.bfloat16), mixed_loc, preferred_element_type=jnp.float32).astype(jnp.bfloat16)
        back_all = lax.all_to_all(back_loc, 'lat', 2, 4, tiled=True)
        wave_loc = jnp.einsum('sctrm,rmj->sctj', back_all, inv_dft, preferred_element_type=jnp.float32).astype(jnp.bfloat16)
        wave_grid = lax.all_to_all(wave_loc, 'lon', 3, 1, tiled=True)
        return field_in + jax.nn.gelu(wave_grid.astype(jnp.float32), approximate=True)

    return jax.shard_map(local_layer, mesh=mesh, in_specs=(grid_spec, P('lat', None, None), P('lat', None, None), P('lon', None, None, None)), out_specs=grid_spec, check_vma=False)
```

profile of v0, /device:TPU:1, one launch (start us, length us, event | category | flops | bytes accessed | tf_op | source)
XLA Modules:
  0.0 709.4 jit_solution(3109157627945303014)
XLA Ops:
  2.6 17.6 %copy.42 = bf16[8,256,24,24]{3,2,0,1:T(8,128)(2,1)} copy(bf16[8,256,24,24]{1,3,2,0:T(8,128)(2,1)S(1)} %convert_element_type.87) | data formatting | bytes 4718592 | tf_op jit(solution)/shard_map/convert_element_type | solution.py:27
  20.2 19.2 %reshape.196 = bf16[16,2,36864]{2,1,0:T(2,128)(2,1)} reshape(bf16[256,8,24,24]{3,2,1,0:T(8,128)(2,1)} %bitcast.113) | data formatting | bytes 4718592
  49.0 33.2 %all-to-all-done = bf16[16,2,36864]{2,1,0:T(2,128)(2,1)S(1)} async-done(((bf16[16,2,36864]{2,1,0:T(2,128)(2,1)}), bf16[16,2,36864]{2,1,0:T(2,128)(2,1)S(1)}, u32[]{:S(2)}, u32[]{:S(2)}) %all-to-all-start) | async-done | bytes 2359328 | tf_op jit(solution)/shard_map/all_to_all | solution.py:28
  82.3 18.5 %reshape.197 = bf16[256,8,24,24]{3,2,1,0:T(8,128)(2,1)} reshape(bf16[16,2,36864]{2,1,0:T(2,128)(2,1)S(1)} %all-to-all-done) | data formatting | bytes 4718592
  100.8 23.0 %copy.44 = bf16[8,16,24,16,24]{4,3,2,1,0:T(8,128)(2,1)} copy(bf16[8,16,24,16,24]{4,2,0,1,3:T(8,128)(2,1)} %bitcast.114) | data formatting | bytes 4718592 | tf_op jit(solution)/shard_map/all_to_all | solution.py:28
  123.8 16.1 %reshape.186 = bf16[8,16,24,384,1]{3,2,1,0,4:T(8,128)(2,1)S(1)} reshape(bf16[8,16,24,16,24]{4,3,2,1,0:T(8,128)(2,1)} %copy.44) | data formatting | bytes 4718592 | tf_op jit(solution)/shard_map/all_to_all | solution.py:28
  142.0 12.7 %copy.45 = bf16[8,16,24,2,128]{2,1,0,3,4:T(8,128)(2,1)} copy(bf16[8,16,24,2,128]{4,2,1,0,3:T(8,128)(2,1)} %fusion.11) | data formatting | bytes 3145728 | tf_op jit(solution)/shard_map/convert_element_type | solution.py:29
  154.8 12.7 %reshape.198 = bf16[8,2,49152]{2,1,0:T(2,128)(2,1)} reshape(bf16[128,2,8,16,24]{4,3,2,1,0:T(8,128)(2,1)} %bitcast.120) | data formatting | bytes 3145728
  173.7 19.2 %all-to-all-done.1 = bf16[8,2,49152]{2,1,0:T(2,128)(2,1)S(1)} async-done(((bf16[8,2,49152]{2,1,0:T(2,128)(2,1)}), bf16[8,2,49152]{2,1,0:T(2,128)(2,1)S(1)}, u32[]{:S(2)}, u32[]{:S(2)}) %all-to-all-start.1) | async-done | bytes 1572896 | tf_op jit(solution)/shard_map/all_to_all | solution.py:30
  193.0 13.2 %reshape.199 = bf16[128,2,8,16,24]{4,3,2,1,0:T(8,128)(2,1)} reshape(bf16[8,2,49152]{2,1,0:T(2,128)(2,1)S(1)} %all-to-all-done.1) | data formatting | bytes 3145728
  206.2 20.1 %copy.47 = bf16[8,16,8,24,2,16]{3,2,1,4,0,5:T(8,128)(2,1)} copy(bf16[8,16,8,24,2,16]{3,1,0,4,5,2:T(8,128)(2,1)} %bitcast.123) | data formatting | bytes 3145728 | tf_op jit(solution)/shard_map/all_to_all | solution.py:30
  238.0 15.0 %copy.48 = bf16[8,16,128,2,16]{1,3,0,4,2:T(2,128)(2,1)} copy(bf16[8,16,128,2,16]{2,1,3,0,4:T(8,128)(2,1)S(1)} %fusion.12) | data formatting | bytes 2097152 | tf_op jit(solution)/shard_map/convert_element_type | solution.py:31
  253.0 11.2 %reshape.200 = bf16[16,2,16384]{2,1,0:T(2,128)(2,1)} reshape(bf16[128,16,8,2,16]{4,3,2,1,0:T(2,128)(2,1)} %bitcast.121) | data formatting | bytes 2097152
  291.8 26.1 %copy.49 = bf16[8,16,128,2,16]{4,2,3,1,0:T(8,128)(2,1)} copy(bf16[8,16,128,2,16]{1,3,0,4,2:T(2,128)(2,1)} %bitcast.124) | data formatting | bytes 2097152 | tf_op jit(solution)/shard_map/all_to_all | solution.py:32
  317.9 16.2 %copy.50 = bf16[8,16,16,8,2,16]{2,1,5,4,0,3:T(8,128)(2,1)} copy(bf16[8,16,16,8,2,16]{5,3,1,4,2,0:T(8,128)(2,1)} %bitcast.125) | data formatting | bytes 2097152 | tf_op jit(solution)/shard_map/all_to_all | solution.py:32
  334.2 10.1 %reshape.188 = bf16[8,256,8,2,16,1]{1,4,3,0,2,5:T(8,128)(2,1)S(1)} reshape(bf16[8,16,16,8,2,16]{2,1,5,4,0,3:T(8,128)(2,1)} %copy.50) | data formatting | bytes 2097152 | tf_op jit(solution)/shard_map/all_to_all | solution.py:32
  348.4 18.7 %copy.53 = bf16[8,256,8,2,16]{4,3,0,2,1:T(2,128)(2,1)} copy(bf16[8,256,8,2,16]{1,4,3,0,2:T(8,128)(2,1)} %fusion.13) | data formatting | bytes 2097152 | tf_op jit(solution)/shard_map/convert_element_type | solution.py:37
  367.1 10.4 %reshape.202 = bf16[16,2,16384]{2,1,0:T(2,128)(2,1)S(1)} reshape(bf16[256,8,8,2,16]{4,3,2,1,0:T(2,128)(2,1)} %bitcast.122) | data formatting | bytes 2097152
  377.6 20.8 %all_to_all.99 = bf16[16,2,16384]{2,1,0:T(2,128)(2,1)S(1)} all-to-all(bf16[16,2,16384]{2,1,0:T(2,128)(2,1)S(1)} %reshape.202), channel_id=1, replica_groups=mesh['member'=1,'lon'=16,'lat'=8] {'lon'}, dimensions={0} | all-to-all | bytes 2097152 | tf_op jit(solution)/shard_map/all_to_all | solution.py:38
  405.8 9.8 %copy.76 = bf16[8,16,16,8,2,16]{5,3,1,4,2,0:T(8,128)(2,1)} copy(bf16[8,16,16,8,2,16]{5,4,0,3,2,1:T(2,128)(2,1)} %bitcast.126) | data formatting | bytes 2097152 | tf_op jit(solution)/shard_map/all_to_all | solution.py:38
  424.9 22.7 %copy.56 = bf16[8,16,192,2,16]{1,3,0,4,2:T(2,128)(2,1)} copy(bf16[8,16,192,2,16]{2,1,3,0,4:T(8,128)(2,1)S(1)} %convert_bitcast_fusion) | data formatting | bytes 3145728 | tf_op jit(solution)/shard_map/convert_element_type | solution.py:39
  447.6 14.9 %reshape.204 = bf16[8,2,49152]{2,1,0:T(2,128)(2,1)} reshape(bf16[192,16,8,2,16]{4,3,2,1,0:T(2,128)(2,1)} %bitcast.115) | data formatting | bytes 3145728
  470.0 18.8 %all-to-all-done.4 = bf16[8,2,49152]{2,1,0:T(2,128)(2,1)S(1)} async-done(((bf16[8,2,49152]{2,1,0:T(2,128)(2,1)}), bf16[8,2,49152]{2,1,0:T(2,128)(2,1)S(1)}, u32[]{:S(2)}, u32[]{:S(2)}) %all-to-all-start.4) | async-done | bytes 1572896 | tf_op jit(solution)/shard_map/all_to_all | solution.py:40
  488.8 10.3 %reshape.205 = bf16[192,16,8,2,16]{4,3,2,1,0:T(2,128)(2,1)} reshape(bf16[8,2,49152]{2,1,0:T(2,128)(2,1)S(1)} %all-to-all-done.4) | data formatting | bytes 3145728
  499.1 38.7 %copy.57 = bf16[8,16,8,24,2,16]{5,2,3,4,1,0:T(8,128)(2,1)} copy(bf16[8,16,8,24,2,16]{1,4,0,5,3,2:T(2,128)(2,1)} %bitcast.116) | data formatting | bytes 3145728 | tf_op jit(solution)/shard_map/all_to_all | solution.py:40
  537.8 14.4 %all_to_all.91 = bf16[8,16,24,2,128]{4,2,3,1,0:T(8,128)(2,1)} reshape(bf16[8,16,24,2,8,16]{5,4,2,3,1,0:T(8,128)(2,1)} %bitcast.117) | data formatting | bytes 3145728 | tf_op jit(solution)/shard_map/all_to_all | solution.py:40
  554.7 17.6 %copy.58 = bf16[8,16,24,384]{2,1,0,3:T(8,128)(2,1)} copy(bf16[8,16,24,384]{3,2,1,0:T(8,128)(2,1)S(1)} %bitcast_convert_fusion) | data formatting | bytes 4718592 | tf_op jit(solution)/shard_map/convert_element_type | solution.py:41
  572.2 18.1 %reshape.206 = bf16[16,2,36864]{2,1,0:T(2,128)(2,1)S(1)} reshape(bf16[384,8,16,24]{3,2,1,0:T(8,128)(2,1)} %bitcast.118) | data formatting | bytes 4718592
  590.3 36.4 %all_to_all.100 = bf16[16,2,36864]{2,1,0:T(2,128)(2,1)} all-to-all(bf16[16,2,36864]{2,1,0:T(2,128)(2,1)S(1)} %reshape.206), channel_id=1, replica_groups=mesh['member'=1,'lon'=16,'lat'=8] {'lon'}, dimensions={0} | all-to-all | bytes 4718592 | tf_op jit(solution)/shard_map/all_to_all | solution.py:42
  626.8 19.2 %reshape.207 = bf16[384,8,16,24]{3,2,1,0:T(8,128)(2,1)} reshape(bf16[16,2,36864]{2,1,0:T(2,128)(2,1)} %all_to_all.100) | data formatting | bytes 4718592
  645.9 31.0 %copy.59 = f32[8,16,24,16,24]{1,3,4,2,0:T(8,128)} copy(bf16[8,16,24,16,24]{2,1,0,4,3:T(8,128)(2,1)} %bitcast.119) | data formatting | bytes 7077888 | tf_op jit(solution)/shard_map/convert_element_type | solution.py:43
  676.9 26.3 %reshape.171 = f32[8,256,24,24]{1,3,2,0:T(8,128)} reshape(f32[8,16,16,24,24]{2,1,4,3,0:T(8,128)} %bitcast.112) | data formatting | bytes 9437184 | tf_op jit(solution)/shard_map/convert_element_type | solution.py:43
  (30 shorter events, 95.3 us)
Async XLA Ops:
  39.4 42.8 %all-to-all-start = ((bf16[16,2,36864]{2,1,0:T(2,128)(2,1)}), bf16[16,2,36864]{2,1,0:T(2,128)(2,1)S(1)}, u32[]{:S(2)}, u32[]{:S(2)}) async-start(bf16[16,2,36864]{2,1,0:T(2,128)(2,1)} %reshape.196), calls=%async_computation | async-start | bytes 4718592 | tf_op jit(solution)/shard_map/all_to_all | solution.py:28
  154.8 17.8 %copy-start.1 = (u32[128]{0:T(128)S(1)}, u32[128]{0:T(128)}, u32[]{:S(2)}) copy-start(u32[128]{0:T(128)} %constant.27) | copy-start | bytes 1540
  167.4 25.5 %all-to-all-start.1 = ((bf16[8,2,49152]{2,1,0:T(2,128)(2,1)}), bf16[8,2,49152]{2,1,0:T(2,128)(2,1)S(1)}, u32[]{:S(2)}, u32[]{:S(2)}) async-start(bf16[8,2,49152]{2,1,0:T(2,128)(2,1)} %reshape.198), calls=%async_computation.1 | async-start | bytes 3145728 | tf_op jit(solution)/shard_map/all_to_all | solution.py:30
  253.0 15.6 %copy-start = (u32[128]{0:T(128)S(1)}, u32[128]{0:T(128)}, u32[]{:S(2)}) copy-start(u32[128]{0:T(128)} %constant.35) | copy-start | bytes 1540
  264.3 20.0 %all-to-all-start.2 = ((bf16[16,2,16384]{2,1,0:T(2,128)(2,1)}), bf16[16,2,16384]{2,1,0:T(2,128)(2,1)S(1)}, u32[]{:S(2)}, u32[]{:S(2)}) async-start(bf16[16,2,16384]{2,1,0:T(2,128)(2,1)} %reshape.200), calls=%async_computation.2 | async-start | bytes 2097152 | tf_op jit(solution)/shard_map/all_to_all | solution.py:32
  462.6 26.2 %all-to-all-start.4 = ((bf16[8,2,49152]{2,1,0:T(2,128)(2,1)}), bf16[8,2,49152]{2,1,0:T(2,128)(2,1)S(1)}, u32[]{:S(2)}, u32[]{:S(2)}) async-start(bf16[8,2,49152]{2,1,0:T(2,128)(2,1)} %reshape.204), calls=%async_computation.4 | async-start | bytes 3145728 | tf_op jit(solution)/shard_map/all_to_all | solution.py:40
where the time goes:
time: 720 us; the launch traced here: 709 us
  local copies, waits for them, and re-layouts  521 us (72%)
  waiting for transfers between devices  79.8 us (11%)
  blocking collectives  57.2 us (8%)
  starting transfers between devices  24.1 us (3%)
  matrix products  12.9 us (2%)
  other arithmetic  12.7 us (2%)
    unnamed x17, local copies, waits for them, and re-layouts  163 us
    convert_element_type x2, local copies, waits for them, and re-layouts, local_layer(): wave_grid.astype(jnp.float32)  57.3 us
    all_to_all x2, local copies, waits for them, and re-layouts, local_layer(): back_all = lax.all_to_all(back_loc, 'lat', 2, 4, tiled=True)  53.1 us
    all_to_all x3, local copies, waits for them, and re-layouts, local_layer(): coef_chan = lax.all_to_all(coef_loc, 'lon', 2, 1, tiled=True)  52.4 us
    all_to_all x2, local copies, waits for them, and re-layouts, local_layer(): lon_full = lax.all_to_all(grid_bf, 'lon', 1, 3, tiled=True)  39.1 us
    all_to_all x1, blocking collectives, local_layer(): wave_grid = lax.all_to_all(wave_loc, 'lon', 3, 1, tiled=True)  36.4 us
    all_to_all x1, waiting for transfers between devices, local_layer(): lon_full = lax.all_to_all(grid_bf, 'lon', 1, 3, tiled=True)  33.2 us
    all_to_all x2, local copies, waits for them, and re-layouts, local_layer(): spec_loc = lax.all_to_all(spec_all, 'lat', 4, 2, tiled=True)  29.7 us
  transfers between devices with their start and end apart: 4, of which 4 were waited for; matrix products, arithmetic and copies ran while one was open for 1% of the time, Pallas kernels for 0%

commit v1 on v0

v1 whole, which is shorter than its diff:
```python
import math
import numpy as np
import jax
import jax.numpy as jnp
from jax import lax
from jax.experimental import pallas as pl
from jax.experimental.pallas import tpu as pltpu
from jax.sharding import PartitionSpec as P

MESH = pl.DeviceIdType.MESH
F32 = jnp.float32
BF16 = jnp.bfloat16

SAMPLES = 8
LON = 16
LAT = 8
ROWS = 576
CHUNK_T = 4
CHUNKS = 6
CROWS = CHUNK_T * 24
TS = 40
LS = 24
W_SLOTS = 8

PEERS = [(2, 2), (2, 1), (2, 3), (1, 2), (3, 2), (2, 0), (0, 2), (1, 1), (3, 3), (1, 3), (3, 1), (1, 0), (0, 1), (3, 0), (0, 3)]


def dft_matrices():
    lon_ids = np.arange(384)
    waves = np.arange(128)
    phase = np.float32(2.0 * math.pi / 384) * ((lon_ids[:, None] * waves[None, :]) % 384).astype(np.float32)
    cos_val, sin_val = np.cos(phase), np.sin(phase)
    weight = np.where(waves == 0, 1.0, 2.0).astype(np.float32)
    fwd = np.stack([cos_val, -sin_val])
    inv = np.stack([weight * cos_val, -weight * sin_val])
    out = []
    for tab in (fwd, inv):
        tab = tab.reshape(2, 16, 24, 16, 8)
        full = np.zeros((8, 2, 2, 16, 16, 2, 24), np.float32)
        part = tab.transpose(4, 0, 3, 1, 2)
        for tt in range(2):
            full[:, tt, :, :, :, tt, :] = part
        out.append(full.reshape(512, 768))
    return out[0].astype(jnp.bfloat16), np.ascontiguousarray(out[1].T).astype(jnp.bfloat16)


def kernel(x_hbm, ft_hbm, it_hbm, w_hbm, dfwd, dinv, y_hbm,
           xf, xs, ra, sp, rb, t1, cf, rc, t2, wb, ws, fs, gs, fb, ib, t3, sd, rd, s2, rebuf, ys,
           x_sem, tab_sem, w_sem, a_send, a_recv, b_send, b_recv, c_send, c_recv, d_send, d_recv,
           e_send, e_recv, f_send, f_recv):
    lon = lax.axis_index('lon')
    lat = lax.axis_index('lat')
    half = lax.rem(lon, 2)
    core = lax.rem(lat, 2)
    quarter = 2 * half + core
    sample = lon // 2

    def dev(n, t):
        return dict(device_id=(0, n, t), device_id_type=MESH)

    def lon_peer(dz, dy):
        return lax.rem(lon // 4 + dz, 4) * 4 + lax.rem(lax.rem(lon, 4) + dy, 4)

    def lat_peer(d):
        return lax.rem(lat + d, LAT)

    def quad(tq):
        return (lon // 2) * 2 + tq // 2, (lat // 2) * 2 + tq % 2

    def rows(ch, size=CROWS, off=0):
        return pl.ds(pl.multiple_of(ch * CROWS + off, 16), size)

    lanes_half = pl.ds(pl.multiple_of(half * 128, 128), 128)

    for ch in range(CHUNKS):
        pltpu.make_async_copy(x_hbm.at[:, pl.ds(ch * CROWS, CROWS)], xf.at[:, pl.ds(ch * CROWS, CROWS)], x_sem.at[ch]).start()
    fwd_load = pltpu.make_async_copy(ft_hbm.at[:, lat], fs, tab_sem.at[0])
    inv_load = pltpu.make_async_copy(it_hbm.at[:, lat], gs, tab_sem.at[1])
    fwd_load.start()
    inv_load.start()

    def degree(idx):
        return jnp.where(idx < 16, quarter * 16 + idx, (7 - quarter) * 16 + idx - 16)

    def w_load(idx):
        slot = lax.rem(idx, W_SLOTS)
        return pltpu.make_async_copy(w_hbm.at[degree(idx)], ws.at[slot], w_sem.at[slot])

    for idx in range(W_SLOTS):
        w_load(jnp.int32(idx)).start()

    rc[...] = jnp.zeros_like(rc)
    rd[...] = jnp.zeros_like(rd)

    bar = pltpu.get_barrier_semaphore()
    for dz, dy in PEERS:
        pl.semaphore_signal(bar, inc=1, **dev(lon_peer(dz, dy), lat))
    for d in range(1, LAT):
        pl.semaphore_signal(bar, inc=1, **dev(lon, lat_peer(d)))
    pl.semaphore_signal(bar, inc=1, **dev((lon // 2) * 2 + 1 - half, (lat // 2) * 2 + 1 - core))
    pl.semaphore_wait(bar, 15 + 7 + 1)

    def send_a(ch, _):
        pltpu.make_async_copy(xf.at[:, rows(ch)], xf.at[:, rows(ch)], x_sem.at[ch]).wait()
        for s in range(SAMPLES):
            for h in range(2):
                xs[2 * s + h, rows(ch), :] = xf[s, rows(ch), h * 128:(h + 1) * 128].astype(BF16)
        for dz, dy in PEERS:
            peer = lon_peer(dz, dy)
            pltpu.make_async_remote_copy(xs.at[peer, rows(ch)], ra.at[lon, rows(ch)], a_send.at[ch], a_recv.at[ch],
                                         **dev(peer, lat)).start()
        pltpu.make_async_copy(xs.at[lon, rows(ch)], ra.at[lon, rows(ch)], a_recv.at[ch]).start()
        return 0

    lax.fori_loop(0, CHUNKS, send_a, 0)

    fwd_load.wait()
    inv_load.wait()

    def prep_tables(i, _):
        fb[i] = fs[i].T.astype(BF16)
        ib[i] = gs[i].astype(BF16)
        return 0

    lax.fori_loop(0, 16, prep_tables, 0)

    def prep_weights(idx, _):
        w_load(idx).wait()
        slot = lax.rem(idx, W_SLOTS)
        for ri in range(2):
            for it in range(2):
                wb[idx, :, ri * 256 + it * 128: ri * 256 + (it + 1) * 128] = ws[slot, pl.ds(2 * it + ri, 256, stride=4), :].astype(BF16)

        @pl.when(idx + W_SLOTS < 32)
        def _():
            w_load(idx + W_SLOTS).start()

        return 0

    def take_b(ch):
        chunk = pl.ds(ch * CHUNK_T, CHUNK_T)
        pltpu.make_async_copy(rb.at[:, chunk], rb.at[:, chunk], b_recv.at[ch]).wait()

        def one(kk, _):
            for tt in range(CHUNK_T):
                row = pl.multiple_of((kk * 24 + ch * CHUNK_T + tt) * TS, 8)
                t1[pl.ds(row, 32), :] = rb[kk, ch * CHUNK_T + tt].astype(F32)
            return 0

        lax.fori_loop(0, LAT, one, 0)

    def dft(ch, _):
        lax.fori_loop(ch * 6, jnp.minimum(ch * 6 + 6, 32), prep_weights, 0)
        pltpu.make_async_copy(ra.at[:, rows(ch)], ra.at[:, rows(ch)], a_recv.at[ch]).wait()
        rhs = jnp.concatenate([ra[:, rows(ch, 48, a * 48), :].reshape(768, 128) for a in range(2)], axis=1)
        out = jnp.dot(dfwd[...], rhs, preferred_element_type=F32)
        for a in range(2):
            sp[:, pl.ds(ch * CHUNK_T + 2 * a, 2)] = out[:, a * 128:(a + 1) * 128].astype(BF16).reshape(8, 2, 32, 128)
        chunk = pl.ds(ch * CHUNK_T, CHUNK_T)
        for d in range(1, LAT):
            peer = lat_peer(d)
            pltpu.make_async_remote_copy(sp.at[peer, chunk], rb.at[lat, chunk], b_send.at[ch], b_recv.at[ch],
                                         **dev(lon, peer)).start()
        pltpu.make_async_copy(sp.at[lat, chunk], rb.at[lat, chunk], b_recv.at[ch]).start()

        @pl.when(ch > 0)
        def _():
            take_b(ch - 1)

        return 0

    lax.fori_loop(0, CHUNKS, dft, 0)
    take_b(CHUNKS - 1)

    def legendre(i, _):
        rhs = jnp.concatenate([t1[pl.ds(i, 192, stride=TS), :], t1[pl.ds(16 + i, 192, stride=TS), :]], axis=1).astype(BF16)
        cf[i] = jnp.dot(fb[i], rhs, preferred_element_type=F32).astype(BF16)
        return 0

    lax.fori_loop(0, 16, legendre, 0, unroll=4)

    for b in range(7, -1, -1):
        tq, lohi, n = (b, 0, 2 * b + 2) if b < 4 else (7 - b, 1, 2 * b + 2)
        src = cf.at[pl.ds(0, n), pl.ds(16 * b, 16)]
        dst = rc.at[pl.ds((quarter * 2 + lohi) * 16, n)]

        @pl.when(quarter == tq)
        def _():
            pltpu.make_async_copy(src, dst, c_recv).start()

        @pl.when(quarter != tq)
        def _():
            pltpu.make_async_remote_copy(src, dst, c_send, c_recv, **dev(*quad(tq))).start()

    pltpu.make_async_copy(rc.at[pl.ds(0, 72)], rc.at[pl.ds(0, 72)], c_recv).wait()

    def take_c(u, _):
        for ri in range(2):
            t2[ri, pl.ds(pl.multiple_of(u * LS, 8), 16), :] = rc[u, :, ri * 128:(ri + 1) * 128].astype(F32)
        return 0

    lax.fori_loop(0, 128, take_c, 0, unroll=4)

    def mix(idx, lohi):
        r = idx - lohi * 16

        def part(ri):
            return jnp.concatenate([jnp.concatenate([
                t2[ri, pl.ds(((2 * hs + cs) * 2 + lohi) * 16 * LS + r, 16, stride=LS), :] for hs in range(2)], axis=1)
                for cs in range(2)], axis=0)

        re, im = part(0), part(1)
        lhs = jnp.concatenate([jnp.concatenate([re, -im], axis=1), jnp.concatenate([im, re], axis=1)], axis=0).astype(BF16)
        out = lax.dot_general(lhs, wb[idx], (((1,), (1,)), ((), ())), preferred_element_type=F32)
        for ri in range(2):
            for oh in range(2):
                t3[ri * 2 + oh, pl.ds(lohi * 32 * LS + r, 32, stride=LS), :] = out[ri * 32:(ri + 1) * 32, oh * 128:(oh + 1) * 128]

    for lohi in (1, 0):
        def mix_step(idx, _, lohi=lohi):
            mix(idx, lohi)
            return 0

        lax.fori_loop(lohi * 16, lohi * 16 + 16, mix_step, 0, unroll=4)

        def pack_d(i, _, lohi=lohi):
            for oh in range(2):
                for cs in range(2):
                    for ri in range(2):
                        row = pl.multiple_of(lohi * 32 * LS + (cs * 16 + i) * LS, 8)
                        sd[((oh * 2 + cs) * 2 + lohi) * 16 + i, :, ri * 128:(ri + 1) * 128] = t3[ri * 2 + oh, pl.ds(row, 16), :].astype(BF16)
            return 0

        lax.fori_loop(0, 16, pack_d, 0)

        for qq in range(4):
            b = qq if lohi == 0 else 7 - qq
            n = 2 * b + 2

            @pl.when(quarter == qq)
            def _():
                for tq in range(4):
                    src = sd.at[pl.ds((tq * 2 + lohi) * 16, n)]
                    dst = rd.at[pl.ds(0, n), pl.ds(16 * b, 16)]
                    if tq == qq:
                        pltpu.make_async_copy(src, dst, d_recv).start()
                    else:
                        pltpu.make_async_remote_copy(src, dst, d_send, d_recv, **dev(*quad(tq))).start()

    pltpu.make_async_copy(rc.at[pl.ds(0, 72)], rc.at[pl.ds(0, 72)], d_recv).wait()

    def inverse(i, _):
        out = jnp.dot(ib[i], rd[i], preferred_element_type=F32)
        t1[pl.ds(i, 192, stride=TS), :] = out[:, :128]
        t1[pl.ds(16 + i, 192, stride=TS), :] = out[:, 128:]
        return 0

    lax.fori_loop(0, 16, inverse, 0, unroll=4)

    def send_e(ch, _):
        chunk = pl.ds(ch * CHUNK_T, CHUNK_T)

        def one(kk, _):
            for tt in range(CHUNK_T):
                row = pl.multiple_of((kk * 24 + ch * CHUNK_T + tt) * TS, 8)
                s2[kk, ch * CHUNK_T + tt] = t1[pl.ds(row, 32), :].astype(BF16)
            return 0

        lax.fori_loop(0, LAT, one, 0)
        for d in range(1, LAT):
            peer = lat_peer(d)
            pltpu.make_async_remote_copy(s2.at[peer, chunk], rebuf.at[lat, chunk], e_send.at[ch], e_recv.at[ch],
                                         **dev(lon, peer)).start()
        pltpu.make_async_copy(s2.at[lat, chunk], rebuf.at[lat, chunk], e_recv.at[ch]).start()
        return 0

    lax.fori_loop(0, CHUNKS, send_e, 0)

    def idft(ch, _):
        chunk = pl.ds(ch * CHUNK_T, CHUNK_T)
        pltpu.make_async_copy(rebuf.at[:, chunk], rebuf.at[:, chunk], e_recv.at[ch]).wait()
        rhs = jnp.concatenate([rebuf[:, pl.ds(ch * CHUNK_T + 2 * a, 2)].reshape(512, 128) for a in range(2)], axis=1)
        out = jnp.dot(dinv[...], rhs, preferred_element_type=F32)
        for a in range(2):
            ys[:, rows(ch, 48, a * 48), :] = out[:, a * 128:(a + 1) * 128].astype(BF16).reshape(16, 48, 128)
        for dz, dy in PEERS:
            peer = lon_peer(dz, dy)
            pltpu.make_async_remote_copy(ys.at[peer, rows(ch)], y_hbm.at[sample, rows(ch), lanes_half], f_send, f_recv,
                                         **dev(peer, lat)).start()
        pltpu.make_async_copy(ys.at[lon, rows(ch)], y_hbm.at[sample, rows(ch), lanes_half], f_recv).start()
        return 0

    lax.fori_loop(0, CHUNKS, idft, 0)

    def drain(ch, _):
        chunk = pl.ds(ch * CHUNK_T, CHUNK_T)
        pltpu.make_async_copy(xs.at[pl.ds(0, 15), rows(ch)], xs.at[pl.ds(0, 15), rows(ch)], a_send.at[ch]).wait()
        pltpu.make_async_copy(sp.at[pl.ds(0, 7), chunk], sp.at[pl.ds(0, 7), chunk], b_send.at[ch]).wait()
        pltpu.make_async_copy(s2.at[pl.ds(0, 7), chunk], s2.at[pl.ds(0, 7), chunk], e_send.at[ch]).wait()
        return 0

    lax.fori_loop(0, CHUNKS, drain, 0)
    for tq in range(4):
        @pl.when(quarter == tq)
        def _():
            n = 72 - 18
            pltpu.make_async_copy(rc.at[pl.ds(0, n)], rc.at[pl.ds(0, n)], c_send).wait()
            pltpu.make_async_copy(rc.at[pl.ds(0, n)], rc.at[pl.ds(0, n)], d_send).wait()
    pltpu.make_async_copy(ys.at[pl.ds(0, 15)], ys.at[pl.ds(0, 15)], f_send).wait()
    pltpu.make_async_copy(y_hbm, y_hbm, f_recv).wait()


def solution(mesh):
    grid_spec = P('member', None, 'lat', 'lon')
    dfwd, dinv = dft_matrices()

    def local_layer(field_in, fwd_table, inv_table, mix_weights):
        rows_view = field_in.transpose(0, 2, 3, 1).reshape(SAMPLES, ROWS, 256)
        ft = fwd_table.transpose(0, 2, 1).reshape(16, 8, 192, 128)
        it = inv_table.transpose(0, 2, 1).reshape(16, 8, 192, 128)
        w = mix_weights.reshape(128, 256, 2, 128, 2).transpose(0, 1, 2, 4, 3).reshape(128, 1024, 128)
        dma = pltpu.SemaphoreType.DMA
        y = pl.pallas_call(
            kernel,
            out_shape=jax.ShapeDtypeStruct((SAMPLES, ROWS, 256), BF16),
            in_specs=[pl.BlockSpec(memory_space=pl.ANY)] * 4 + [pl.BlockSpec(memory_space=pltpu.VMEM)] * 2,
            out_specs=pl.BlockSpec(memory_space=pl.ANY),
            scratch_shapes=[
                pltpu.VMEM((SAMPLES, ROWS, 256), F32),
                pltpu.VMEM((LON, ROWS, 128), BF16),
                pltpu.VMEM((LON, ROWS, 128), BF16),
                pltpu.VMEM((LAT, 24, 32, 128), BF16),
                pltpu.VMEM((LAT, 24, 32, 128), BF16),
                pltpu.VMEM((192 * TS, 128), F32),
                pltpu.VMEM((16, 128, 256), BF16),
                pltpu.VMEM((128, 16, 256), BF16),
                pltpu.VMEM((2, 128 * LS, 128), F32),
                pltpu.VMEM((32, 256, 512), BF16),
                pltpu.VMEM((W_SLOTS, 1024, 128), F32),
                pltpu.VMEM((16, 192, 128), F32),
                pltpu.VMEM((16, 192, 128), F32),
                pltpu.VMEM((16, 128, 192), BF16),
                pltpu.VMEM((16, 192, 128), BF16),
                pltpu.VMEM((4, 64 * LS, 128), F32),
                pltpu.VMEM((128, 16, 256), BF16),
                pltpu.VMEM((16, 128, 256), BF16),
                pltpu.VMEM((LAT, 24, 32, 128), BF16),
                pltpu.VMEM((LAT, 24, 32, 128), BF16),
                pltpu.VMEM((LON, ROWS, 128), BF16),
                dma((CHUNKS,)), dma((2,)), dma((W_SLOTS,)),
                dma((CHUNKS,)), dma((CHUNKS,)), dma((CHUNKS,)), dma((CHUNKS,)),
                dma, dma, dma, dma,
                dma((CHUNKS,)), dma((CHUNKS,)), dma, dma,
            ],
            compiler_params=pltpu.CompilerParams(collective_id=0, has_side_effects=True, vmem_limit_bytes=67043328),
        )(rows_view, ft, it, w, jnp.asarray(dfwd), jnp.asarray(dinv))
        y = y.reshape(SAMPLES, 24, 24, 256).transpose(0, 3, 1, 2)
        return field_in + jax.nn.gelu(y.astype(F32), approximate=True)

    return jax.shard_map(local_layer, mesh=mesh, in_specs=(grid_spec, P(), P(), P()), out_specs=grid_spec, check_vma=False)
```

time: 720 us -> 111 us (0.15); the launches traced: 709 us -> 111 us
  local copies, waits for them, and re-layouts: 521 us -> 0 us
  Pallas kernels: 0 us -> 104 us
  waiting for transfers between devices: 79.8 us -> 0 us
  blocking collectives: 57.2 us -> 0 us
  starting transfers between devices: 24.1 us -> 0 us
  matrix products: 12.9 us -> 0 us
    all_to_all x11 -> x0, local copies, waits for them, and re-layouts: 191 us -> none  [the longest x2 53.1 us: local_layer(): back_all = lax.all_to_all(back_loc, 'lat', 2, 4, tiled=True)]
    unnamed x17 -> x0, local copies, waits for them, and re-layouts: 163 us -> none
    convert_element_type x8 -> x0, local copies, waits for them, and re-layouts: 162 us -> none  [the longest x2 57.3 us: local_layer(): wave_grid.astype(jnp.float32)]
    pallas_call x0 -> x1, Pallas kernels: none -> 104 us  [local_layer(): pl.pallas_call(kernel, out_shape=jax.ShapeDtypeStruct((SAMPLES, ROWS, 256...]
    all_to_all x4 -> x0, waiting for transfers between devices: 79.8 us -> none  [the longest x1 33.2 us: local_layer(): lon_full = lax.all_to_all(grid_bf, 'lon', 1, 3, tiled=True)]
    all_to_all x2 -> x0, blocking collectives: 57.2 us -> none  [the longest x1 36.4 us: local_layer(): wave_grid = lax.all_to_all(wave_loc, 'lon', 3, 1, tiled=True)]
    all_to_all x4 -> x0, starting transfers between devices: 24.1 us -> none  [the longest x1 8.77 us: local_layer(): lon_full = lax.all_to_all(grid_bf, 'lon', 1, 3, tiled=True)]
    dot_general x5 -> x0, matrix products: 12.9 us -> none  [the longest x1 4.15 us: local_layer(): jnp.einsum('loqir,silrm->solqm', w_block, coef_chan, preferred_element_ty...]
  transfers between devices with their start and end apart: 4 -> 0, of which waited for: 4 -> 0; matrix products, arithmetic and copies ran while one was open for 1% -> 0% of each run, Pallas kernels for 0% -> 0%
where the time goes in v1:
time: 111 us
  Pallas kernels  104 us (94%)
  other arithmetic  6.97 us (6%)
    pallas_call x1, Pallas kernels, local_layer(): pl.pallas_call(kernel, out_shape=jax.ShapeDtypeStruct((SAMPLES, ROWS, 256...  104 us
    add x1, other arithmetic, local_layer(): return field_in + jax.nn.gelu(y.astype(F32), approximate=True)  6.97 us

profile of v1, /device:TPU:1, one launch (start us, length us, event | category | flops | bytes accessed | tf_op | source)
XLA Modules:
  0.0 111.2 jit_solution(9370442976333450894)
XLA Ops:
  0.0 104.2 %shard_map.64 = bf16[8,576,256]{2,1,0:T(8,128)(2,1)} custom-call(f32[8,576,256]{2,1,0:T(8,128)} %bitcast.20, f32[16,8,192,128]{3,2,1,0:T(8,128)} %bitcast.21, f32[16,8,192,128]{3,2,1,0:T(8,128)} %bitcast.22, f32[128,1024,128]{2,1,0:T(8,128)} %bitcast.8.w_hbm, bf16[512,768]{1,0:T(8,128)(2,1)} %constant.12.clone.dfwd, bf16[768,512]{1,0:T(8,128)(2,1)} %constant.13.clone.dinv), custom_call_target="tpu_custom_call" | custom-call | tf_op jit(solution)/shard_map/pallas_call | solution.py:323
  104.3 7.0 %fusion.7 = f32[8,256,24,24]{1,3,2,0:T(8,128)} fusion(f32[8,256,24,24]{1,3,2,0:T(8,128)} %param.6, bf16[8,24,24,256]{3,2,1,0:T(8,128)(2,1)} %bitcast.23), kind=kLoop, calls=%fused_computation.8 | loop fusion | flops 11796480 | bytes 11796480 | tf_op jit(solution)/shard_map/add | solution.py:358

commit v2 on v1

--- a/solution.py
+++ b/solution.py
@@ -15,13 +15,14 @@
 LON = 16
 LAT = 8
 ROWS = 576
-CHUNK_T = 4
-CHUNKS = 6
+CHUNK_T = 2
+CHUNKS = 12
 CROWS = CHUNK_T * 24
 TS = 40
 LS = 24
 W_SLOTS = 8
 
+EVEN = [(2, 2), (1, 1), (3, 3), (1, 3), (3, 1), (2, 0), (0, 2), (0, 0)]
 PEERS = [(2, 2), (2, 1), (2, 3), (1, 2), (3, 2), (2, 0), (0, 2), (1, 1), (3, 3), (1, 3), (3, 1), (1, 0), (0, 1), (3, 0), (0, 3)]
 
 
@@ -44,75 +45,108 @@
     return out[0].astype(jnp.bfloat16), np.ascontiguousarray(out[1].T).astype(jnp.bfloat16)
 
 
-def kernel(x_hbm, ft_hbm, it_hbm, w_hbm, dfwd, dinv, y_hbm,
-           xf, xs, ra, sp, rb, t1, cf, rc, t2, wb, ws, fs, gs, fb, ib, t3, sd, rd, s2, rebuf, ys,
+def kernel(x_hbm, ft_hbm, it_hbm, w_hbm, dfwd, dinv, o_hbm,
+           xf, xs, ra, sp, rb, t1, cf, rc, t2, wb, ws, fs, gs, fb, ib, t3, sd, rd, s2, rebuf, ys, yr,
            x_sem, tab_sem, w_sem, a_send, a_recv, b_send, b_recv, c_send, c_recv, d_send, d_recv,
-           e_send, e_recv, f_send, f_recv):
+           e_send, e_recv, f_send, f_recv, o_sem):
     lon = lax.axis_index('lon')
     lat = lax.axis_index('lat')
-    half = lax.rem(lon, 2)
+    z, y = lon // 4, lax.rem(lon, 4)
+    group = lax.rem(z + y, 2)
+    sample = group * 4 + z
+    half = y // 2
     core = lax.rem(lat, 2)
     quarter = 2 * half + core
-    sample = lon // 2
 
     def dev(n, t):
         return dict(device_id=(0, n, t), device_id_type=MESH)
 
     def lon_peer(dz, dy):
-        return lax.rem(lon // 4 + dz, 4) * 4 + lax.rem(lax.rem(lon, 4) + dy, 4)
+        return lax.rem(z + dz, 4) * 4 + lax.rem(y + dy, 4)
 
     def lat_peer(d):
         return lax.rem(lat + d, LAT)
 
     def quad(tq):
-        return (lon // 2) * 2 + tq // 2, (lat // 2) * 2 + tq % 2
+        return z * 4 + lax.rem(y, 2) + 2 * (tq // 2), (lat // 2) * 2 + tq % 2
 
     def rows(ch, size=CROWS, off=0):
         return pl.ds(pl.multiple_of(ch * CROWS + off, 16), size)
 
     lanes_half = pl.ds(pl.multiple_of(half * 128, 128), 128)
 
-    for ch in range(CHUNKS):
-        pltpu.make_async_copy(x_hbm.at[:, pl.ds(ch * CROWS, CROWS)], xf.at[:, pl.ds(ch * CROWS, CROWS)], x_sem.at[ch]).start()
-    fwd_load = pltpu.make_async_copy(ft_hbm.at[:, lat], fs, tab_sem.at[0])
-    inv_load = pltpu.make_async_copy(it_hbm.at[:, lat], gs, tab_sem.at[1])
-    fwd_load.start()
-    inv_load.start()
-
-    def degree(idx):
-        return jnp.where(idx < 16, quarter * 16 + idx, (7 - quarter) * 16 + idx - 16)
-
-    def w_load(idx):
-        slot = lax.rem(idx, W_SLOTS)
-        return pltpu.make_async_copy(w_hbm.at[degree(idx)], ws.at[slot], w_sem.at[slot])
-
-    for idx in range(W_SLOTS):
-        w_load(jnp.int32(idx)).start()
-
-    rc[...] = jnp.zeros_like(rc)
-    rd[...] = jnp.zeros_like(rd)
+    def x_load(tg, ch):
+        part = (pl.ds(tg * 4, 4), rows(ch))
+        return pltpu.make_async_copy(x_hbm.at[part], xf.at[part], x_sem.at[tg * CHUNKS + ch])
+
+    def start_x(n, _):
+        x_load(n // CHUNKS, lax.rem(n, CHUNKS)).start()
+        return 0
 
     bar = pltpu.get_barrier_semaphore()
     for dz, dy in PEERS:
         pl.semaphore_signal(bar, inc=1, **dev(lon_peer(dz, dy), lat))
     for d in range(1, LAT):
         pl.semaphore_signal(bar, inc=1, **dev(lon, lat_peer(d)))
-    pl.semaphore_signal(bar, inc=1, **dev((lon // 2) * 2 + 1 - half, (lat // 2) * 2 + 1 - core))
+    pl.semaphore_signal(bar, inc=1, **dev(lon_peer(0, 2), (lat // 2) * 2 + 1 - core))
+
+    lax.fori_loop(0, 2 * CHUNKS, start_x, 0)
+    fwd_load = pltpu.make_async_copy(ft_hbm.at[:, lat], fs, tab_sem.at[0])
+    inv_load = pltpu.make_async_copy(it_hbm.at[:, lat], gs, tab_sem.at[1])
+    fwd_load.start()
+    inv_load.start()
+
+    def degree(idx):
+        return jnp.where(idx < 16, quarter * 16 + idx, (7 - quarter) * 16 + idx - 16)
+
+    def w_load(idx):
+        slot = lax.rem(idx, W_SLOTS)
+        return pltpu.make_async_copy(w_hbm.at[degree(idx)], ws.at[slot], w_sem.at[slot])
+
+    for idx in range(W_SLOTS):
+        w_load(jnp.int32(idx)).start()
+
+    for i in range(2, 16):
+        rd[i, 0:16 * (i // 2), :] = jnp.zeros((16 * (i // 2), 256), BF16)
+
+    def convert(tg):
+        def body(ch, _):
+            x_load(tg, ch).wait()
+            for zz in range(4):
+                for h in range(2):
+                    xs[4 * zz + 2 * h + (zz + tg) % 2, rows(ch), :] = xf[4 * tg + zz, rows(ch), h * 128:(h + 1) * 128].astype(BF16)
+            return 0
+
+        lax.fori_loop(0, CHUNKS, body, 0)
+
+    def send_a(tg):
+        shift = lax.rem(group + tg, 2)
+
+        def body(ch, _):
+            for dz, dy in EVEN:
+                peer = lon_peer(dz, dy + shift)
+                src, dst = xs.at[peer, rows(ch)], ra.at[lon, rows(ch)]
+
+                def remote():
+                    pltpu.make_async_remote_copy(src, dst, a_send.at[ch], a_recv.at[ch], **dev(peer, lat)).start()
+
+                if (dz, dy) != (0, 0):
+                    remote()
+                else:
+                    pl.when(shift != 0)(remote)
+
+                    @pl.when(shift == 0)
+                    def _():
+                        pltpu.make_async_copy(src, dst, a_recv.at[ch]).start()
+            return 0
+
+        lax.fori_loop(0, CHUNKS, body, 0)
+
+    convert(0)
     pl.semaphore_wait(bar, 15 + 7 + 1)
-
-    def send_a(ch, _):
-        pltpu.make_async_copy(xf.at[:, rows(ch)], xf.at[:, rows(ch)], x_sem.at[ch]).wait()
-        for s in range(SAMPLES):
-            for h in range(2):
-                xs[2 * s + h, rows(ch), :] = xf[s, rows(ch), h * 128:(h + 1) * 128].astype(BF16)
-        for dz, dy in PEERS:
-            peer = lon_peer(dz, dy)
-            pltpu.make_async_remote_copy(xs.at[peer, rows(ch)], ra.at[lon, rows(ch)], a_send.at[ch], a_recv.at[ch],
-                                         **dev(peer, lat)).start()
-        pltpu.make_async_copy(xs.at[lon, rows(ch)], ra.at[lon, rows(ch)], a_recv.at[ch]).start()
-        return 0
-
-    lax.fori_loop(0, CHUNKS, send_a, 0)
+    send_a(0)
+    convert(1)
+    send_a(1)
 
     fwd_load.wait()
     inv_load.wait()
@@ -150,12 +184,10 @@
         lax.fori_loop(0, LAT, one, 0)
 
     def dft(ch, _):
-        lax.fori_loop(ch * 6, jnp.minimum(ch * 6 + 6, 32), prep_weights, 0)
+        lax.fori_loop(ch * 3, jnp.minimum(ch * 3 + 3, 32), prep_weights, 0)
         pltpu.make_async_copy(ra.at[:, rows(ch)], ra.at[:, rows(ch)], a_recv.at[ch]).wait()
-        rhs = jnp.concatenate([ra[:, rows(ch, 48, a * 48), :].reshape(768, 128) for a in range(2)], axis=1)
-        out = jnp.dot(dfwd[...], rhs, preferred_element_type=F32)
-        for a in range(2):
-            sp[:, pl.ds(ch * CHUNK_T + 2 * a, 2)] = out[:, a * 128:(a + 1) * 128].astype(BF16).reshape(8, 2, 32, 128)
+        out = jnp.dot(dfwd[...], ra[:, rows(ch), :].reshape(768, 128), preferred_element_type=F32)
+        sp[:, pl.ds(ch * CHUNK_T, CHUNK_T)] = out.astype(BF16).reshape(8, 2, 32, 128)
         chunk = pl.ds(ch * CHUNK_T, CHUNK_T)
         for d in range(1, LAT):
             peer = lat_peer(d)
@@ -186,20 +218,28 @@
 
         @pl.when(quarter == tq)
         def _():
-            pltpu.make_async_copy(src, dst, c_recv).start()
+            pltpu.make_async_copy(src, dst, c_recv.at[lohi]).start()
 
         @pl.when(quarter != tq)
         def _():
-            pltpu.make_async_remote_copy(src, dst, c_send, c_recv, **dev(*quad(tq))).start()
-
-    pltpu.make_async_copy(rc.at[pl.ds(0, 72)], rc.at[pl.ds(0, 72)], c_recv).wait()
-
-    def take_c(u, _):
-        for ri in range(2):
-            t2[ri, pl.ds(pl.multiple_of(u * LS, 8), 16), :] = rc[u, :, ri * 128:(ri + 1) * 128].astype(F32)
-        return 0
-
-    lax.fori_loop(0, 128, take_c, 0, unroll=4)
+            pltpu.make_async_remote_copy(src, dst, c_send, c_recv.at[lohi], **dev(*quad(tq))).start()
+
+    def take_c(lohi):
+        for qq in range(4):
+            n = 4 * (2 * qq + 2 if lohi == 0 else 16 - 2 * qq)
+
+            @pl.when(quarter == qq)
+            def _():
+                pltpu.make_async_copy(rc.at[pl.ds(0, n)], rc.at[pl.ds(0, n)], c_recv.at[lohi]).wait()
+
+        def one(i, _):
+            for sq in range(4):
+                u = (sq * 2 + lohi) * 16 + i
+                for ri in range(2):
+                    t2[ri, pl.ds(pl.multiple_of(u * LS, 8), 16), :] = rc[u, :, ri * 128:(ri + 1) * 128].astype(F32)
+            return 0
+
+        lax.fori_loop(0, 16, one, 0)
 
     def mix(idx, lohi):
         r = idx - lohi * 16
@@ -217,6 +257,8 @@
                 t3[ri * 2 + oh, pl.ds(lohi * 32 * LS + r, 32, stride=LS), :] = out[ri * 32:(ri + 1) * 32, oh * 128:(oh + 1) * 128]
 
     for lohi in (1, 0):
+        take_c(lohi)
+
         def mix_step(idx, _, lohi=lohi):
             mix(idx, lohi)
             return 0
@@ -279,18 +321,28 @@
     def idft(ch, _):
         chunk = pl.ds(ch * CHUNK_T, CHUNK_T)
         pltpu.make_async_copy(rebuf.at[:, chunk], rebuf.at[:, chunk], e_recv.at[ch]).wait()
-        rhs = jnp.concatenate([rebuf[:, pl.ds(ch * CHUNK_T + 2 * a, 2)].reshape(512, 128) for a in range(2)], axis=1)
-        out = jnp.dot(dinv[...], rhs, preferred_element_type=F32)
-        for a in range(2):
-            ys[:, rows(ch, 48, a * 48), :] = out[:, a * 128:(a + 1) * 128].astype(BF16).reshape(16, 48, 128)
+        out = jnp.dot(dinv[...], rebuf[:, chunk].reshape(512, 128), preferred_element_type=F32)
+        ys[:, rows(ch), :] = out.astype(BF16).reshape(16, 48, 128)
+        arrived = f_recv.at[group * CHUNKS + ch]
         for dz, dy in PEERS:
             peer = lon_peer(dz, dy)
-            pltpu.make_async_remote_copy(ys.at[peer, rows(ch)], y_hbm.at[sample, rows(ch), lanes_half], f_send, f_recv,
+            pltpu.make_async_remote_copy(ys.at[peer, rows(ch)], yr.at[sample, rows(ch), lanes_half], f_send, arrived,
                                          **dev(peer, lat)).start()
-        pltpu.make_async_copy(ys.at[lon, rows(ch)], y_hbm.at[sample, rows(ch), lanes_half], f_recv).start()
+        pltpu.make_async_copy(ys.at[lon, rows(ch)], yr.at[sample, rows(ch), lanes_half], arrived).start()
         return 0
 
     lax.fori_loop(0, CHUNKS, idft, 0)
+
+    def finish_rows(n, _):
+        tg, ch = n // CHUNKS, lax.rem(n, CHUNKS)
+        part = (pl.ds(tg * 4, 4), rows(ch))
+        pltpu.make_async_copy(yr.at[part], yr.at[part], f_recv.at[n]).wait()
+        for k in range(4):
+            xf[tg * 4 + k, rows(ch), :] += jax.nn.gelu(yr[tg * 4 + k, rows(ch), :].astype(F32), approximate=True)
+        pltpu.make_async_copy(xf.at[part], o_hbm.at[part], o_sem).start()
+        return 0
+
+    lax.fori_loop(0, 2 * CHUNKS, finish_rows, 0)
 
     def drain(ch, _):
         chunk = pl.ds(ch * CHUNK_T, CHUNK_T)
@@ -307,7 +359,7 @@
             pltpu.make_async_copy(rc.at[pl.ds(0, n)], rc.at[pl.ds(0, n)], c_send).wait()
             pltpu.make_async_copy(rc.at[pl.ds(0, n)], rc.at[pl.ds(0, n)], d_send).wait()
     pltpu.make_async_copy(ys.at[pl.ds(0, 15)], ys.at[pl.ds(0, 15)], f_send).wait()
-    pltpu.make_async_copy(y_hbm, y_hbm, f_recv).wait()
+    pltpu.make_async_copy(xf, o_hbm, o_sem).wait()
 
 
 def solution(mesh):
@@ -320,9 +372,9 @@
         it = inv_table.transpose(0, 2, 1).reshape(16, 8, 192, 128)
         w = mix_weights.reshape(128, 256, 2, 128, 2).transpose(0, 1, 2, 4, 3).reshape(128, 1024, 128)
         dma = pltpu.SemaphoreType.DMA
-        y = pl.pallas_call(
+        out = pl.pallas_call(
             kernel,
-            out_shape=jax.ShapeDtypeStruct((SAMPLES, ROWS, 256), BF16),
+            out_shape=jax.ShapeDtypeStruct((SAMPLES, ROWS, 256), F32),
             in_specs=[pl.BlockSpec(memory_space=pl.ANY)] * 4 + [pl.BlockSpec(memory_space=pltpu.VMEM)] * 2,
             out_specs=pl.BlockSpec(memory_space=pl.ANY),
             scratch_shapes=[
@@ -347,14 +399,14 @@
                 pltpu.VMEM((LAT, 24, 32, 128), BF16),
                 pltpu.VMEM((LAT, 24, 32, 128), BF16),
                 pltpu.VMEM((LON, ROWS, 128), BF16),
-                dma((CHUNKS,)), dma((2,)), dma((W_SLOTS,)),
+                pltpu.VMEM((SAMPLES, ROWS, 256), BF16),
+                dma((2 * CHUNKS,)), dma((2,)), dma((W_SLOTS,)),
                 dma((CHUNKS,)), dma((CHUNKS,)), dma((CHUNKS,)), dma((CHUNKS,)),
-                dma, dma, dma, dma,
-                dma((CHUNKS,)), dma((CHUNKS,)), dma, dma,
+                dma, dma((2,)), dma, dma,
+                dma((CHUNKS,)), dma((CHUNKS,)), dma, dma((2 * CHUNKS,)), dma,
             ],
             compiler_params=pltpu.CompilerParams(collective_id=0, has_side_effects=True, vmem_limit_bytes=67043328),
         )(rows_view, ft, it, w, jnp.asarray(dfwd), jnp.asarray(dinv))
-        y = y.reshape(SAMPLES, 24, 24, 256).transpose(0, 3, 1, 2)
-        return field_in + jax.nn.gelu(y.astype(F32), approximate=True)
+        return out.reshape(SAMPLES, 24, 24, 256).transpose(0, 3, 1, 2)
 
     return jax.shard_map(local_layer, mesh=mesh, in_specs=(grid_spec, P(), P(), P()), out_specs=grid_spec, check_vma=False)

time: 111 us -> 126 us (1.14)
  Pallas kernels: 104 us -> 121 us
  other arithmetic: 6.97 us -> 0 us
  local copies, waits for them, and re-layouts: 0 us -> 4.9 us
    pallas_call x1, Pallas kernels: 104 us -> 121 us  [local_layer(): pl.pallas_call(kernel, out_shape=jax.ShapeDtypeStruct((SAMPLES, ROWS, 256...]
    add x1 -> x0, other arithmetic: 6.97 us -> none  [local_layer(): return field_in + jax.nn.gelu(y.astype(F32), approximate=True)]
    unnamed x0 -> x1, local copies, waits for them, and re-layouts: none -> 4.9 us
where the time goes in v2:
time: 126 us
  Pallas kernels  121 us (96%)
  local copies, waits for them, and re-layouts  4.9 us (4%)
    pallas_call x1, Pallas kernels, local_layer(): pl.pallas_call(kernel, out_shape=jax.ShapeDtypeStruct((SAMPLES, ROWS, 256...  121 us
    unnamed x1, local copies, waits for them, and re-layouts  4.9 us

profile of v2, /device:TPU:1, one launch (start us, length us, event | category | flops | bytes accessed | tf_op | source)
XLA Modules:
  0.0 125.8 jit_solution(9353897444337378726)
XLA Ops:
  0.0 120.9 %shard_map.64 = f32[8,576,256]{2,1,0:T(8,128)} custom-call(f32[8,576,256]{2,1,0:T(8,128)} %bitcast.20, f32[16,8,192,128]{3,2,1,0:T(8,128)} %bitcast.18, f32[16,8,192,128]{3,2,1,0:T(8,128)} %bitcast.19, f32[128,1024,128]{2,1,0:T(8,128)} %bitcast.8.w_hbm, bf16[512,768]{1,0:T(8,128)(2,1)} %constant.4.clone.dfwd, bf16[768,512]{1,0:T(8,128)(2,1)} %constant.5.clone.dinv), custom_call_target="tpu_custom_call" | custom-call | tf_op jit(solution)/shard_map/pallas_call | solution.py:375
  120.9 4.9 %copy.9 = f32[8,256,24,24]{1,3,2,0:T(8,128)} copy(f32[8,256,24,24]{1,3,2,0:T(8,128)} %bitcast.17) | data formatting | bytes 9437184

commit v3 on v0

v3 whole, which is shorter than its diff:
```python
import math
import numpy as np
import jax
import jax.numpy as jnp
from jax import lax
from jax.experimental import pallas as pl
from jax.experimental.pallas import tpu as pltpu
from jax.sharding import PartitionSpec as P

MESH = pl.DeviceIdType.MESH
F32 = jnp.float32
BF16 = jnp.bfloat16

SAMPLES = 8
LON = 16
LAT = 8
ROWS = 576
CHUNKS = 6
TS = 40
LS = 24
W_SLOTS = 8
GRID = (2, LON, 288, 128)
SPEC = (2, LAT, 12, 32, 128)
A1_EARLY = 4

FAR = sorted(((dz, dy) for dz in range(4) for dy in range(4)), key=lambda d: -min(d[0], 4 - d[0]) - min(d[1], 4 - d[1]))
PEERS = FAR[:-1]


def dft_matrices():
    lon_ids = np.arange(384)
    waves = np.arange(128)
    phase = np.float32(2.0 * math.pi / 384) * ((lon_ids[:, None] * waves[None, :]) % 384).astype(np.float32)
    cos_val, sin_val = np.cos(phase), np.sin(phase)
    weight = np.where(waves == 0, 1.0, 2.0).astype(np.float32)
    fwd = np.stack([cos_val, -sin_val])
    inv = np.stack([weight * cos_val, -weight * sin_val])
    out = []
    for tab in (fwd, inv):
        tab = tab.reshape(2, 16, 24, 16, 8)
        full = np.zeros((8, 2, 2, 16, 16, 2, 24), np.float32)
        part = tab.transpose(4, 0, 3, 1, 2)
        for tt in range(2):
            full[:, tt, :, :, :, tt, :] = part
        out.append(full.reshape(512, 768))
    return out[0].astype(jnp.bfloat16), np.ascontiguousarray(out[1].T).astype(jnp.bfloat16)


def kernel(x_hbm, ft_hbm, it_hbm, w_hbm, dfwd_hbm, dinv_hbm, o_hbm,
           xf, xs, ra, sp, rb, t1, cf, rc, t2, wb, ws, fs, gs, fb, ib, t3, sd, rd, s2, rebuf, ys, yr, dfwd, dinv,
           x_sem, tab_sem, w_sem, a_send, a_recv, b_send, b_recv, c_send, c_recv, d_send, d_recv,
           e_send, e_recv, f_send, f_recv, o_sem):
    lon = lax.axis_index('lon')
    lat = lax.axis_index('lat')
    z, y = lon // 4, lax.rem(lon, 4)
    core = lax.rem(lat, 2)
    block = jnp.where(core == 0, y, 7 - y)

    def dev(n, t):
        return dict(device_id=(0, n, t), device_id_type=MESH)

    def lon_peer(dz, dy):
        return lax.rem(z + dz, 4) * 4 + lax.rem(y + dy, 4)

    def lat_peer(d):
        return lax.rem(lat + d, LAT)

    def mixer(tq, tc):
        return dev(z * 4 + tq, (lat // 2) * 2 + tc)

    def wide(ch):
        return pl.ds(pl.multiple_of(ch * 96, 16), 96)

    def rows(ch):
        return pl.ds(pl.multiple_of(ch * 48, 16), 48)

    def pair(ch):
        return pl.ds(ch * 2, 2)

    def await_copy(ref, sem):
        pltpu.make_async_copy(ref, ref, sem).wait()

    def swap(a, b):
        low = lax.broadcasted_iota(jnp.int32, a.shape, 1) < 64
        return jnp.where(low, a, pltpu.roll(b, 64, 1)), jnp.where(low, pltpu.roll(a, 64, 1), b)

    bar = pltpu.get_barrier_semaphore()
    for dz, dy in PEERS:
        pl.semaphore_signal(bar, inc=1, **dev(lon_peer(dz, dy), lat))
    for d in range(1, LAT):
        pl.semaphore_signal(bar, inc=1, **dev(lon, lat_peer(d)))
    for dy in range(1, 4):
        pl.semaphore_signal(bar, inc=1, **dev(lon_peer(0, dy), (lat // 2) * 2 + 1 - core))

    def x_load(g, ch):
        part = (pl.ds(4 * g, 4), wide(ch))
        return pltpu.make_async_copy(x_hbm.at[part], xf.at[part], x_sem.at[g, ch])

    for g in range(2):
        for ch in range(CHUNKS):
            x_load(g, ch).start()
    fwd_load = pltpu.make_async_copy(ft_hbm.at[:, lat], fs, tab_sem.at[0])
    inv_load = pltpu.make_async_copy(it_hbm.at[:, lat], gs, tab_sem.at[1])
    dfwd_load = pltpu.make_async_copy(dfwd_hbm, dfwd, tab_sem.at[2])
    dinv_load = pltpu.make_async_copy(dinv_hbm, dinv, tab_sem.at[3])
    dfwd_load.start()
    fwd_load.start()
    inv_load.start()

    def w_load(idx):
        slot = lax.rem(idx, W_SLOTS)
        return pltpu.make_async_copy(w_hbm.at[block * 16 + idx], ws.at[slot], w_sem.at[slot])

    for idx in range(W_SLOTS):
        w_load(jnp.int32(idx)).start()
    dinv_load.start()

    for g in range(2):
        for i in range(2, 16):
            rd[g, i, 0:16 * (i // 2), :] = jnp.zeros((16 * (i // 2), 128), BF16)

    def convert(g, ch):
        x_load(g, ch).wait()
        for s in range(4):
            for it in range(2):
                lanes = slice(it * 128, (it + 1) * 128)
                parts = [swap(xf[4 * g + s, pl.ds(pl.multiple_of(ch * 96 + tp * 48, 8), 24), lanes],
                              xf[4 * g + s, pl.ds(pl.multiple_of(ch * 96 + tp * 48 + 24, 8), 24), lanes]) for tp in range(2)]
                for odd in range(2):
                    xs[g, 4 * s + 2 * it + odd, rows(ch), :] = jnp.concatenate([parts[0][odd], parts[1][odd]], axis=0).astype(BF16)

    def send_a(g, ch):
        for dz, dy in PEERS:
            peer = lon_peer(dz, dy)
            pltpu.make_async_remote_copy(xs.at[g, peer, rows(ch)], ra.at[g, lon, rows(ch)], a_send.at[g], a_recv.at[g, ch],
                                         **dev(peer, lat)).start()
        pltpu.make_async_copy(xs.at[g, lon, rows(ch)], ra.at[g, lon, rows(ch)], a_recv.at[g, ch]).start()

    def loop(fun, g, start=0, stop=CHUNKS):
        def step(ch, _):
            fun(g, ch)
            return 0

        lax.fori_loop(start, stop, step, 0)

    def convert_send(g, ch):
        convert(g, ch)
        send_a(g, ch)

    pl.semaphore_wait(bar, 15 + 7 + 3)
    loop(convert_send, 0)
    loop(convert_send, 1, 0, A1_EARLY)
    loop(convert, 1, A1_EARLY)

    fwd_load.wait()
    inv_load.wait()

    def prep_tables(i, _):
        fb[i] = jnp.concatenate([fs[i, pl.ds(tt, 96, stride=2), :] for tt in range(2)], axis=0).T.astype(BF16)
        ib[i] = jnp.concatenate([gs[i, pl.ds(tt, 96, stride=2), :] for tt in range(2)], axis=0).astype(BF16)
        return 0

    lax.fori_loop(0, 16, prep_tables, 0)

    def prep_weights(idx, _):
        w_load(idx).wait()
        slot = lax.rem(idx, W_SLOTS)
        for it in range(2):
            both = swap(ws[slot, pl.ds(2 * it, 256, stride=4), :], ws[slot, pl.ds(2 * it + 1, 256, stride=4), :])
            for odd in range(2):
                wb[idx, :, (2 * it + odd) * 128:(2 * it + odd + 1) * 128] = both[odd].astype(BF16)

        @pl.when(idx + W_SLOTS < 16)
        def _():
            w_load(idx + W_SLOTS).start()

        return 0

    def take_b(g, ch):
        await_copy(rb.at[g, :, pair(ch)], b_recv.at[g, ch])

        def one(kk, _):
            for tp in range(2):
                t1[g, pl.ds(pl.multiple_of((kk * 12 + ch * 2 + tp) * TS, 8), 32), :] = rb[g, kk, ch * 2 + tp].astype(F32)
            return 0

        lax.fori_loop(0, LAT, one, 0)

    def dft(g, ch):
        if g == 0:
            lax.fori_loop(ch * 3, jnp.minimum(ch * 3 + 3, 16), prep_weights, 0)
        await_copy(ra.at[g, :, rows(ch)], a_recv.at[g, ch])
        out = jnp.dot(dfwd[...], ra[g, :, rows(ch), :].reshape(768, 128), preferred_element_type=F32)
        sp[g, :, pair(ch)] = out.astype(BF16).reshape(8, 2, 32, 128)
        for d in range(1, LAT):
            peer = lat_peer(d)
            pltpu.make_async_remote_copy(sp.at[g, peer, pair(ch)], rb.at[g, lat, pair(ch)], b_send.at[g], b_recv.at[g, ch],
                                         **dev(lon, peer)).start()
        pltpu.make_async_copy(sp.at[g, lat, pair(ch)], rb.at[g, lat, pair(ch)], b_recv.at[g, ch]).start()

    def legendre(g):
        def step(i, _):
            rhs = jnp.concatenate(swap(t1[g, pl.ds(i, 96, stride=TS), :], t1[g, pl.ds(16 + i, 96, stride=TS), :]), axis=0).astype(BF16)
            cf[g, i] = jnp.dot(fb[i], rhs, preferred_element_type=F32).astype(BF16)
            return 0

        lax.fori_loop(0, 16, step, 0, unroll=4)

    def send_c(g):
        for b in range(7, -1, -1):
            tq, tc = (b, 0) if b < 4 else (7 - b, 1)
            n = 2 * b + 2
            src = cf.at[g, pl.ds(0, n), pl.ds(16 * b, 16)]
            dst = rc.at[g, pl.ds((y * 2 + core) * 16, n)]

            @pl.when(block == b)
            def _():
                pltpu.make_async_copy(src, dst, c_recv.at[g]).start()

            @pl.when(block != b)
            def _():
                pltpu.make_async_remote_copy(src, dst, c_send.at[g], c_recv.at[g], **mixer(tq, tc)).start()

    def mix(g):
        for b in range(8):
            @pl.when(block == b)
            def _():
                await_copy(rc.at[g, pl.ds(0, 16 * (b + 1))], c_recv.at[g])

        def take_c(i, _):
            for sq in range(8):
                t2[pl.ds(pl.multiple_of((sq * 16 + i) * LS, 8), 16), :] = rc[g, sq * 16 + i].astype(F32)
            return 0

        lax.fori_loop(0, 16, take_c, 0)

        def step(r, _):
            straight, crossed = [], []
            for cs in range(2):
                part = [t2[pl.ds((2 * q + cs) * 16 * LS + r, 16, stride=LS), :] for q in range(4)]
                low = lax.broadcasted_iota(jnp.int32, (16, 128), 1) < 64
                straight.append(jnp.concatenate([jnp.where(low, p, -p) for p in part], axis=1))
                crossed.append(jnp.concatenate([pltpu.roll(p, 64, 1) for p in part], axis=1))
            lhs = jnp.concatenate(straight + crossed, axis=0).astype(BF16)
            out = lax.dot_general(lhs, wb[r], (((1,), (1,)), ((), ())), preferred_element_type=F32)
            for it in range(2):
                both = swap(out[:32, it * 128:(it + 1) * 128], out[32:, it * 128:(it + 1) * 128])
                for odd in range(2):
                    t3[2 * it + odd, pl.ds(r, 32, stride=LS), :] = both[odd]
            return 0

        lax.fori_loop(0, 16, step, 0, unroll=8)

        def pack(i, _):
            for tq in range(4):
                for tc in range(2):
                    sd[g, (tq * 2 + tc) * 16 + i] = t3[tq, pl.ds(pl.multiple_of((tc * 16 + i) * LS, 8), 16), :].astype(BF16)
            return 0

        lax.fori_loop(0, 16, pack, 0)
        for b in range(8):
            n = 2 * b + 2
            own = (b, 0) if b < 4 else (7 - b, 1)

            @pl.when(block == b)
            def _():
                for tq in range(4):
                    for tc in range(2):
                        src = sd.at[g, pl.ds((tq * 2 + tc) * 16, n)]
                        dst = rd.at[g, pl.ds(0, n), pl.ds(16 * b, 16)]
                        if (tq, tc) == own:
                            pltpu.make_async_copy(src, dst, d_recv.at[g]).start()
                        else:
                            pltpu.make_async_remote_copy(src, dst, d_send.at[g], d_recv.at[g], **mixer(tq, tc)).start()

    def inverse(g):
        await_copy(rc.at[g, pl.ds(0, 72)], d_recv.at[g])

        def step(i, _):
            out = jnp.dot(ib[i], rd[g, i], preferred_element_type=F32)
            both = swap(out[:96], out[96:])
            for ri in range(2):
                t1[g, pl.ds(ri * 16 + i, 96, stride=TS), :] = both[ri]
            return 0

        lax.fori_loop(0, 16, step, 0, unroll=4)

    def send_e(g, ch):
        def one(kk, _):
            for tp in range(2):
                s2[g, kk, ch * 2 + tp] = t1[g, pl.ds(pl.multiple_of((kk * 12 + ch * 2 + tp) * TS, 8), 32), :].astype(BF16)
            return 0

        lax.fori_loop(0, LAT, one, 0)
        for d in range(1, LAT):
            peer = lat_peer(d)
            pltpu.make_async_remote_copy(s2.at[g, peer, pair(ch)], rebuf.at[g, lat, pair(ch)], e_send.at[g], e_recv.at[g, ch],
                                         **dev(lon, peer)).start()
        pltpu.make_async_copy(s2.at[g, lat, pair(ch)], rebuf.at[g, lat, pair(ch)], e_recv.at[g, ch]).start()

    def idft(g, ch):
        await_copy(rebuf.at[g, :, pair(ch)], e_recv.at[g, ch])
        out = jnp.dot(dinv[...], rebuf[g, :, pair(ch)].reshape(512, 128), preferred_element_type=F32)
        ys[g, :, rows(ch), :] = out.astype(BF16).reshape(16, 48, 128)
        for dz, dy in PEERS:
            peer = lon_peer(dz, dy)
            pltpu.make_async_remote_copy(ys.at[g, peer, rows(ch)], yr.at[g, lon, rows(ch)], f_send.at[g], f_recv.at[g, ch],
                                         **dev(peer, lat)).start()
        pltpu.make_async_copy(ys.at[g, lon, rows(ch)], yr.at[g, lon, rows(ch)], f_recv.at[g, ch]).start()

    def finish_rows(g, ch):
        await_copy(yr.at[g, :, rows(ch)], f_recv.at[g, ch])
        for s in range(4):
            for it in range(2):
                both = swap(yr[g, 4 * s + 2 * it, rows(ch), :].astype(F32), yr[g, 4 * s + 2 * it + 1, rows(ch), :].astype(F32))
                for tt in range(2):
                    val = jax.nn.gelu(both[tt], approximate=True)
                    for tp in range(2):
                        at = pl.ds(pl.multiple_of(ch * 96 + tp * 48 + tt * 24, 8), 24)
                        xf[4 * g + s, at, it * 128:(it + 1) * 128] += val[tp * 24:(tp + 1) * 24]
        part = (pl.ds(4 * g, 4), wide(ch))
        pltpu.make_async_copy(xf.at[part], o_hbm.at[part], o_sem).start()

    dfwd_load.wait()
    loop(dft, 0)
    loop(take_b, 0)
    legendre(0)
    send_c(0)
    loop(send_a, 1, A1_EARLY)
    loop(dft, 1, 0, 3)
    mix(0)
    loop(dft, 1, 3)
    inverse(0)
    loop(send_e, 0, 0, 3)
    loop(take_b, 1)
    legendre(1)
    send_c(1)
    loop(send_e, 0, 3)
    dinv_load.wait()
    loop(idft, 0, 0, 2)
    mix(1)
    loop(idft, 0, 2)
    inverse(1)
    loop(send_e, 1)
    loop(idft, 1)
    loop(finish_rows, 0)
    loop(finish_rows, 1)

    for g in range(2):
        await_copy(xs.at[g, pl.ds(0, 15)], a_send.at[g])
        await_copy(sp.at[g, pl.ds(0, 7)], b_send.at[g])
        await_copy(s2.at[g, pl.ds(0, 7)], e_send.at[g])
        await_copy(ys.at[g, pl.ds(0, 15)], f_send.at[g])
        for b in range(8):
            @pl.when(block == b)
            def _():
                await_copy(rc.at[g, pl.ds(0, 70 - 2 * b)], c_send.at[g])
                await_copy(rc.at[g, pl.ds(0, 14 * (b + 1))], d_send.at[g])
    pltpu.make_async_copy(xf, o_hbm, o_sem).wait()


def solution(mesh):
    grid_spec = P('member', None, 'lat', 'lon')
    dfwd, dinv = dft_matrices()

    def local_layer(field_in, fwd_table, inv_table, mix_weights):
        rows_view = field_in.transpose(0, 2, 3, 1).reshape(SAMPLES, ROWS, 256)
        ft = fwd_table.transpose(0, 2, 1).reshape(16, 8, 192, 128)
        it = inv_table.transpose(0, 2, 1).reshape(16, 8, 192, 128)
        w = mix_weights.reshape(128, 256, 2, 128, 2).transpose(0, 1, 2, 4, 3).reshape(128, 1024, 128)
        dma = pltpu.SemaphoreType.DMA
        out = pl.pallas_call(
            kernel,
            out_shape=pltpu.VMEM((SAMPLES, ROWS, 256), F32),
            in_specs=[pl.BlockSpec(memory_space=pl.ANY)] * 6,
            out_specs=pl.BlockSpec(memory_space=pl.ANY),
            scratch_shapes=[
                pltpu.VMEM((SAMPLES, ROWS, 256), F32),
                pltpu.VMEM(GRID, BF16),
                pltpu.VMEM(GRID, BF16),
                pltpu.VMEM(SPEC, BF16),
                pltpu.VMEM(SPEC, BF16),
                pltpu.VMEM((2, 96 * TS, 128), F32),
                pltpu.VMEM((2, 16, 128, 128), BF16),
                pltpu.VMEM((2, 128, 16, 128), BF16),
                pltpu.VMEM((128 * LS, 128), F32),
                pltpu.VMEM((16, 256, 512), BF16),
                pltpu.VMEM((W_SLOTS, 1024, 128), F32),
                pltpu.VMEM((16, 192, 128), F32),
                pltpu.VMEM((16, 192, 128), F32),
                pltpu.VMEM((16, 128, 192), BF16),
                pltpu.VMEM((16, 192, 128), BF16),
                pltpu.VMEM((4, 32 * LS, 128), F32),
                pltpu.VMEM((2, 128, 16, 128), BF16),
                pltpu.VMEM((2, 16, 128, 128), BF16),
                pltpu.VMEM(SPEC, BF16),
                pltpu.VMEM(SPEC, BF16),
                pltpu.VMEM(GRID, BF16),
                pltpu.VMEM(GRID, BF16),
                pltpu.VMEM((512, 768), BF16),
                pltpu.VMEM((768, 512), BF16),
                dma((2, CHUNKS)), dma((4,)), dma((W_SLOTS,)),
                dma((2,)), dma((2, CHUNKS)), dma((2,)), dma((2, CHUNKS)),
                dma((2,)), dma((2,)), dma((2,)), dma((2,)),
                dma((2,)), dma((2, CHUNKS)), dma((2,)), dma((2, CHUNKS)), dma,
            ],
            compiler_params=pltpu.CompilerParams(collective_id=0, has_side_effects=True, vmem_limit_bytes=56 * 2**20),
        )(rows_view, ft, it, w, jnp.asarray(dfwd), jnp.asarray(dinv))
        return out.reshape(SAMPLES, 24, 24, 256).transpose(0, 3, 1, 2)

    return jax.shard_map(local_layer, mesh=mesh, in_specs=(grid_spec, P(), P(), P()), out_specs=grid_spec, check_vma=False)
```

time: 720 us -> 88.4 us (0.12); the launches traced: 709 us -> 88.1 us
  local copies, waits for them, and re-layouts: 521 us -> 2.19 us
  Pallas kernels: 0 us -> 85.9 us
  waiting for transfers between devices: 79.8 us -> 0 us
  blocking collectives: 57.2 us -> 0 us
  starting transfers between devices: 24.1 us -> 0 us
  matrix products: 12.9 us -> 0 us
  other arithmetic: 12.7 us -> 0 us
    all_to_all x11 -> x0, local copies, waits for them, and re-layouts: 191 us -> none  [the longest x2 53.1 us: local_layer(): back_all = lax.all_to_all(back_loc, 'lat', 2, 4, tiled=True)]
    convert_element_type x8 -> x0, local copies, waits for them, and re-layouts: 162 us -> none  [the longest x2 57.3 us: local_layer(): wave_grid.astype(jnp.float32)]
    unnamed x17 -> x1, local copies, waits for them, and re-layouts: 163 us -> 2.19 us
    pallas_call x0 -> x1, Pallas kernels: none -> 85.9 us  [local_layer(): pl.pallas_call(kernel, out_shape=pltpu.VMEM((SAMPLES, ROWS, 256), F32), i...]
    all_to_all x4 -> x0, waiting for transfers between devices: 79.8 us -> none  [the longest x1 33.2 us: local_layer(): lon_full = lax.all_to_all(grid_bf, 'lon', 1, 3, tiled=True)]
    all_to_all x2 -> x0, blocking collectives: 57.2 us -> none  [the longest x1 36.4 us: local_layer(): wave_grid = lax.all_to_all(wave_loc, 'lon', 3, 1, tiled=True)]
    all_to_all x4 -> x0, starting transfers between devices: 24.1 us -> none  [the longest x1 8.77 us: local_layer(): lon_full = lax.all_to_all(grid_bf, 'lon', 1, 3, tiled=True)]
    dot_general x5 -> x0, matrix products: 12.9 us -> none  [the longest x1 4.15 us: local_layer(): jnp.einsum('loqir,silrm->solqm', w_block, coef_chan, preferred_element_ty...]
  transfers between devices with their start and end apart: 4 -> 0, of which waited for: 4 -> 0; matrix products, arithmetic and copies ran while one was open for 1% -> 0% of each run, Pallas kernels for 0% -> 0%
where the time goes in v3:
time: 88.4 us; the launch traced here: 88.1 us
  Pallas kernels  85.9 us (97%)
  local copies, waits for them, and re-layouts  2.19 us (2%)
    pallas_call x1, Pallas kernels, local_layer(): pl.pallas_call(kernel, out_shape=pltpu.VMEM((SAMPLES, ROWS, 256), F32), i...  85.9 us
    unnamed x1, local copies, waits for them, and re-layouts  2.19 us

profile of v3, /device:TPU:1, one launch (start us, length us, event | category | flops | bytes accessed | tf_op | source)
XLA Modules:
  0.0 88.1 jit_solution(5787189469176741457)
XLA Ops:
  0.0 85.9 %shard_map.64 = f32[8,576,256]{2,1,0:T(8,128)S(1)} custom-call(f32[8,576,256]{2,1,0:T(8,128)} %bitcast.20, f32[16,8,192,128]{3,2,1,0:T(8,128)} %bitcast.18, f32[16,8,192,128]{3,2,1,0:T(8,128)} %bitcast.19, f32[128,1024,128]{2,1,0:T(8,128)} %bitcast.8.w_hbm, bf16[512,768]{1,0:T(8,128)(2,1)} %constant.4.clone.dfwd_hbm, bf16[768,512]{1,0:T(8,128)(2,1)} %constant.5.clone.dinv_hbm), custom_call_target="tpu_custom_call" | custom-call | tf_op jit(solution)/shard_map/pallas_call | solution.py:372
  85.9 2.2 %copy.9 = f32[8,256,24,24]{1,3,2,0:T(8,128)} copy(f32[8,256,24,24]{1,3,2,0:T(8,128)S(1)} %bitcast.17) | data formatting | bytes 9437184
